TPU v7x, 32 devices: a whole 2x2x4 slice. The times are simulated.
32 devices in a mesh: dp: 8 (over z, x), tensor: 4 (over y, core).
Axes of the slice: x: 2, y: 2, z: 4, core: 2. Of those that a mesh axis runs over, the one named last changes fastest.
Arguments:
- noise: float32 [32, 16, 256], P('dp'), may hold values from -6 to 6
- velocity: float32 [32, 16, 256], P('dp'), may hold values from -6 to 6
- times: float32 [32], P('dp'), may hold values from 0 to 1
- labels: int32 [32], P('dp'), may hold values from 0 to 999
- step_count: int32 [], replicated, may hold values from 1 to 20
- stem: float32 [3592, 768], P(None, 'dp'), may hold values from -0.5 to 0.5
- stem_first: float32 [3592, 768], P(None, 'dp'), may hold values from -0.00030517578 to 0.00030517578
- stem_second: float32 [3592, 768], P(None, 'dp'), may hold values from 2.0840002e-11 to 3.3344003e-10
- w_in: float32 [2, 768, 9984], P(None, 'dp', 'tensor'), may hold values from -0.21875 to 0.21875
- w_in_first: float32 [2, 768, 9984], P(None, 'dp', 'tensor'), may hold values from -0.00030517578 to 0.00030517578
- w_in_second: float32 [2, 768, 9984], P(None, 'dp', 'tensor'), may hold values from 2.0840002e-11 to 3.3344003e-10
- w_out: float32 [2, 3840, 768], P(None, 'tensor', 'dp'), may hold values from -0.4375 to 0.4375
- w_out_first: float32 [2, 3840, 768], P(None, 'tensor', 'dp'), may hold values from -0.00030517578 to 0.00030517578
- w_out_second: float32 [2, 3840, 768], P(None, 'tensor', 'dp'), may hold values from 2.0840002e-11 to 3.3344003e-10
Outputs:
- loss: float32 [], replicated
- grad_norm: float32 [], replicated
- stem_new: float32 [3592, 768], P(None, 'dp')
- stem_first_new: float32 [3592, 768], P(None, 'dp')
- stem_second_new: float32 [3592, 768], P(None, 'dp')
- stem_low: bfloat16 [3592, 768], P(None, 'dp')
- w_in_new: float32 [2, 768, 9984], P(None, 'dp', 'tensor')
- w_in_first_new: float32 [2, 768, 9984], P(None, 'dp', 'tensor')
- w_in_second_new: float32 [2, 768, 9984], P(None, 'dp', 'tensor')
- w_in_low: bfloat16 [2, 768, 9984], P(None, 'dp', 'tensor')
- w_out_new: float32 [2, 3840, 768], P(None, 'tensor', 'dp')
- w_out_first_new: float32 [2, 3840, 768], P(None, 'tensor', 'dp')
- w_out_second_new: float32 [2, 3840, 768], P(None, 'tensor', 'dp')
- w_out_low: bfloat16 [2, 3840, 768], P(None, 'tensor', 'dp')
All inputs are finite; a program needn't handle non-finite values.
Results may differ from a plain program's by a relative error of at most 0.0071.
Values may be sent and summed in bfloat16 or wider, within the bound.
A program may use at most 192 MiB of HBM per device.

v0:
```python
import math
import jax
import jax.numpy as jnp
from jax import lax
from jax.sharding import PartitionSpec as P

D = 768
H = 12
DH = 64
FF = 3072
CLASSES = 1000
PF = 16
FREQ = 256
GRID = 16
LAYERS = 2
NTOK = 256
CLIP_AT = 1.0
LEARN_RATE = 0.03
BETA_ONE = 0.9
BETA_TWO = 0.999
EPSILON = 1e-08
DECAY = 0.01


def matmul(left, right):
    return jnp.dot(left, right, preferred_element_type=jnp.float32)


def dot_left(left, right):
    return lax.dot_general(
        left, right, (((0,), (0,)), ((), ())), preferred_element_type=jnp.float32
    )


def dot_right(left, right):
    return lax.dot_general(
        left, right, (((1,), (1,)), ((), ())), preferred_element_type=jnp.float32
    )


def normalize(values):
    center = values - jnp.mean(values, axis=-1, keepdims=True)
    spread = jnp.mean(center * center, axis=-1, keepdims=True)
    return center * lax.rsqrt(spread + 1e-06)


def modulate(values, shift, scale):
    return normalize(values) * (1.0 + scale[:, None, :]) + shift[:, None, :]


def positions(grid, width):
    quarter = width // 4
    omega = 1.0 / 10000.0 ** (jnp.arange(quarter, dtype=jnp.float32) / quarter)
    angles = jnp.arange(grid, dtype=jnp.float32)[:, None] * omega[None, :]
    single = jnp.concatenate([jnp.sin(angles), jnp.cos(angles)], axis=1)
    rows_part = jnp.repeat(single, grid, axis=0)
    cols_part = jnp.tile(single, (grid, 1))
    return jnp.concatenate([rows_part, cols_part], axis=1)


def time_features(times, count):
    half = count // 2
    freqs = jnp.exp(-math.log(10000.0) * jnp.arange(half, dtype=jnp.float32) / half)
    angles = 1000.0 * times[:, None] * freqs[None, :]
    return jnp.concatenate([jnp.cos(angles), jnp.sin(angles)], axis=1)


def layout(width):
    parts = lax.axis_size("tensor")
    heads = H // parts
    return (heads, 3 * heads * DH, FF // parts, 6 * width // parts)


def fetch_layer(w_in, w_out, layer):
    return (
        lax.all_gather(w_in[layer].astype(jnp.bfloat16), "dp", axis=0, tiled=True),
        lax.all_gather(w_out[layer].astype(jnp.bfloat16), "dp", axis=1, tiled=True),
    )


def combine(partial_value):
    return lax.psum(partial_value.astype(jnp.bfloat16), "tensor").astype(jnp.float32)


def attention_scores(qkv):
    query, key = (qkv[:, :, :, 0], qkv[:, :, :, 1])
    return jnp.einsum("bnhe,bmhe->bhnm", query, key, preferred_element_type=jnp.float32) * DH ** (
        -0.5
    )


def layer_forward(state, cond_act, win_b, wout_b):
    batch, width = (state.shape[0], state.shape[2])
    heads, qcols, fcols, mcols = layout(width)
    mod_part = matmul(cond_act, win_b[:, qcols + fcols :]).astype(jnp.bfloat16)
    mod = lax.all_gather(mod_part, "tensor", axis=1, tiled=True).astype(jnp.float32)
    pieces = jnp.split(mod, 6, axis=1)
    x_attn = modulate(state, pieces[0], pieces[1]).astype(jnp.bfloat16)
    tokens = x_attn.shape[1]
    x_attn = x_attn.reshape(-1, width)
    qkv = matmul(x_attn, win_b[:, :qcols]).astype(jnp.bfloat16).reshape(batch, tokens, heads, 3, DH)
    scores = attention_scores(qkv)
    total = jax.nn.logsumexp(scores, axis=-1, keepdims=True)
    probs = jnp.exp(scores - total).astype(jnp.bfloat16)
    context = jnp.einsum(
        "bhnm,bmhe->bnhe", probs, qkv[:, :, :, 2], preferred_element_type=jnp.float32
    )
    context = context.astype(jnp.bfloat16).reshape(-1, heads * DH)
    attn = combine(matmul(context, wout_b[: heads * DH]).reshape(batch, tokens, width))
    mid = state + pieces[2][:, None, :] * attn
    x_mlp = modulate(mid, pieces[3], pieces[4]).astype(jnp.bfloat16).reshape(-1, width)
    pre = matmul(x_mlp, win_b[:, qcols : qcols + fcols])
    act = jax.nn.gelu(pre, approximate=True).astype(jnp.bfloat16)
    out = combine(matmul(act, wout_b[heads * DH :]).reshape(batch, tokens, width))
    kept = (state, mod, x_attn, qkv, total, context, attn, mid, x_mlp, pre, act, out)
    return (mid + pieces[5][:, None, :] * out, kept)


def layer_backward(grad, kept, cond_act, win_b, wout_b):
    state, mod, x_attn, qkv, total, context, attn, mid, x_mlp, pre, act, out = kept
    batch, width = (state.shape[0], state.shape[2])
    heads, qcols, fcols, mcols = layout(width)
    tokens = qkv.shape[1]
    pieces = jnp.split(mod, 6, axis=1)
    gate_mlp = jnp.sum(grad * out, axis=1)
    d_out = (pieces[5][:, None, :] * grad).astype(jnp.bfloat16).reshape(-1, width)
    g_fc2 = dot_left(act, d_out)
    d_act = dot_right(d_out, wout_b[heads * DH :])
    gelu_back = jax.vjp(lambda v: jax.nn.gelu(v, approximate=True), pre)[1]
    d_pre = gelu_back(d_act)[0].astype(jnp.bfloat16)
    g_fc1 = dot_left(x_mlp, d_pre)
    d_xmlp = combine(
        dot_right(d_pre, win_b[:, qcols : qcols + fcols]).reshape(batch, tokens, width)
    )
    d_mid, shift_mlp, scale_mlp = jax.vjp(modulate, mid, pieces[3], pieces[4])[1](d_xmlp)
    d_mid = d_mid + grad
    gate_attn = jnp.sum(d_mid * attn, axis=1)
    d_attn = (pieces[2][:, None, :] * d_mid).astype(jnp.bfloat16).reshape(-1, width)
    g_proj = dot_left(context, d_attn)
    d_context = (
        dot_right(d_attn, wout_b[: heads * DH])
        .astype(jnp.bfloat16)
        .reshape(batch, tokens, heads, DH)
    )
    query, key, value = (qkv[:, :, :, 0], qkv[:, :, :, 1], qkv[:, :, :, 2])
    weights_full = jnp.exp(attention_scores(qkv) - total)
    d_probs = jnp.einsum("bnhe,bmhe->bhnm", d_context, value, preferred_element_type=jnp.float32)
    d_value = jnp.einsum(
        "bhnm,bnhe->bmhe",
        weights_full.astype(jnp.bfloat16),
        d_context,
        preferred_element_type=jnp.float32,
    )
    inner = jnp.sum(d_probs * weights_full, axis=-1, keepdims=True)
    d_scores = (weights_full * (d_probs - inner)).astype(jnp.bfloat16)
    d_query = jnp.einsum(
        "bhnm,bmhe->bnhe", d_scores, key, preferred_element_type=jnp.float32
    ) * DH ** (-0.5)
    d_key = jnp.einsum(
        "bhnm,bnhe->bmhe", d_scores, query, preferred_element_type=jnp.float32
    ) * DH ** (-0.5)
    d_qkv = jnp.stack([d_query, d_key, d_value], axis=3).astype(jnp.bfloat16).reshape(-1, qcols)
    g_qkv = dot_left(x_attn, d_qkv)
    d_xattn = combine(dot_right(d_qkv, win_b[:, :qcols]).reshape(batch, tokens, width))
    d_state, shift_attn, scale_attn = jax.vjp(modulate, state, pieces[0], pieces[1])[1](d_xattn)
    d_state = d_state + d_mid
    d_mod = jnp.concatenate(
        [shift_attn, scale_attn, gate_attn, shift_mlp, scale_mlp, gate_mlp], axis=1
    )
    d_mod = lax.dynamic_slice_in_dim(d_mod, lax.axis_index("tensor") * mcols, mcols, 1)
    d_mod = d_mod.astype(jnp.bfloat16)
    g_mod = dot_left(cond_act, d_mod)
    d_cond = dot_right(d_mod, win_b[:, qcols + fcols :])
    return (
        d_state,
        d_cond,
        jnp.concatenate([g_qkv, g_fc1, g_mod], axis=1),
        jnp.concatenate([g_proj, g_fc2], axis=0),
    )


def adamw(weight, first, second, gradient, fix_one, fix_two):
    first = BETA_ONE * first + (1.0 - BETA_ONE) * gradient
    second = BETA_TWO * second + (1.0 - BETA_TWO) * gradient * gradient
    step = first / fix_one / (jnp.sqrt(second / fix_two) + EPSILON) + DECAY * weight
    fresh = weight - LEARN_RATE * step
    return (fresh, first, second, fresh.astype(jnp.bfloat16))


def on_device(
    noise,
    velocity,
    times,
    labels,
    step_count,
    stem,
    stem_first,
    stem_second,
    w_in,
    w_in_first,
    w_in_second,
    w_out,
    w_out_first,
    w_out_second,
):
    parts = lax.axis_size("tensor")
    batch = noise.shape[0]
    gathered = lax.all_gather(stem.astype(jnp.bfloat16), "dp", axis=1, tiled=True)
    offsets = [PF, PF + FREQ, PF + FREQ + D, PF + FREQ + D + CLASSES, PF + FREQ + 3 * D + CLASSES]
    patch, freq_w, time_w, table, final_mod, final_out = jnp.split(gathered, offsets, axis=0)
    tokens = (
        jnp.swapaxes(noise + times[:, None, None] * velocity, 1, 2)
        .reshape(-1, PF)
        .astype(jnp.bfloat16)
    )
    embed = matmul(tokens, patch).reshape(batch, NTOK, D) + positions(GRID, D)[None]
    features = time_features(times, FREQ).astype(jnp.bfloat16)
    time_pre = matmul(features, freq_w)
    hidden = jax.nn.silu(time_pre).astype(jnp.bfloat16)
    onehot = (labels[:, None] == jnp.arange(CLASSES, dtype=jnp.int32)[None, :]).astype(jnp.bfloat16)
    cond = matmul(hidden, time_w) + matmul(onehot, table)
    cond_act = jax.nn.silu(cond).astype(jnp.bfloat16)
    state = embed
    saved = []
    for layer in range(LAYERS):
        win_b, wout_b = fetch_layer(w_in, w_out, layer)
        state, kept = layer_forward(state, cond_act, win_b, wout_b)
        saved.append(kept)
    final = dot_right(cond_act, final_mod)
    x_final = modulate(state, final[:, :D], final[:, D:]).astype(jnp.bfloat16).reshape(-1, D)
    pred = dot_right(x_final, final_out).reshape(batch, NTOK, PF)
    diff = pred - jnp.swapaxes(velocity, 1, 2)
    weight_time = 0.5 + times
    loss_local = jnp.sum(weight_time * jnp.mean(diff * diff, axis=(1, 2)))
    d_pred = (
        (2.0 / (NTOK * PF) * weight_time[:, None, None] * diff).astype(jnp.bfloat16).reshape(-1, PF)
    )
    g_final_out = dot_left(d_pred, x_final)
    d_xfinal = matmul(d_pred, final_out).reshape(batch, NTOK, D)
    grad, final_shift, final_scale = jax.vjp(modulate, state, final[:, :D], final[:, D:])[1](
        d_xfinal
    )
    d_final = jnp.concatenate([final_shift, final_scale], axis=1).astype(jnp.bfloat16)
    g_final_mod = dot_left(d_final, cond_act)
    d_cond_final = matmul(d_final, final_mod)
    d_cond_layers = jnp.zeros((batch, D), jnp.float32)
    in_grads = [None] * LAYERS
    out_grads = [None] * LAYERS
    for layer in reversed(range(LAYERS)):
        win_b, wout_b = (
            lax.all_gather(w_in[layer].astype(jnp.bfloat16), "dp", axis=0, tiled=True),
            lax.all_gather(w_out[layer].astype(jnp.bfloat16), "dp", axis=1, tiled=True),
        )
        grad, d_part, g_in, g_outw = layer_backward(grad, saved[layer], cond_act, win_b, wout_b)
        d_cond_layers = d_cond_layers + d_part
        g_in, g_outw = (
            lax.psum_scatter(g_in, "dp", scatter_dimension=0, tiled=True),
            lax.psum_scatter(g_outw, "dp", scatter_dimension=1, tiled=True),
        )
        in_grads[layer] = g_in
        out_grads[layer] = g_outw
    d_cond_act = lax.psum(d_cond_layers, "tensor") + d_cond_final
    d_cond = jax.vjp(jax.nn.silu, cond)[1](d_cond_act)[0].astype(jnp.bfloat16)
    g_time = dot_left(hidden, d_cond)
    g_table = dot_left(onehot, d_cond)
    d_hidden = dot_right(d_cond, time_w)
    d_time_pre = jax.vjp(jax.nn.silu, time_pre)[1](d_hidden)[0].astype(jnp.bfloat16)
    g_freq = dot_left(features, d_time_pre)
    d_embed = grad.astype(jnp.bfloat16).reshape(-1, D)
    g_patch = dot_left(tokens, d_embed)
    stem_grad = jnp.concatenate(
        [g_patch, g_freq, g_time, g_table, g_final_mod, g_final_out], axis=0
    )
    stem_grad = lax.psum_scatter(stem_grad, "dp", scatter_dimension=1, tiled=True)
    in_stack = jnp.stack(in_grads)
    out_stack = jnp.stack(out_grads)
    squares = (
        jnp.sum(stem_grad * stem_grad) / parts
        + jnp.sum(in_stack * in_stack)
        + jnp.sum(out_stack * out_stack)
    )
    loss, square_total = lax.psum((loss_local / parts, squares), ("dp", "tensor"))
    grad_norm = jnp.sqrt(square_total)
    factor = jnp.minimum(1.0, CLIP_AT / grad_norm)
    steps_done = step_count.astype(jnp.float32)
    fix_one = 1.0 - jnp.power(BETA_ONE, steps_done)
    fix_two = 1.0 - jnp.power(BETA_TWO, steps_done)
    stem_out = adamw(stem, stem_first, stem_second, factor * stem_grad, fix_one, fix_two)
    in_out = adamw(w_in, w_in_first, w_in_second, factor * in_stack, fix_one, fix_two)
    out_out = adamw(w_out, w_out_first, w_out_second, factor * out_stack, fix_one, fix_two)
    return (
        loss,
        grad_norm,
        stem_out[0],
        stem_out[1],
        stem_out[2],
        stem_out[3],
        in_out[0],
        in_out[1],
        in_out[2],
        in_out[3],
        out_out[0],
        out_out[1],
        out_out[2],
        out_out[3],
    )


def solution(mesh):
    in_specs = (
        P("dp", None, None),
        P("dp", None, None),
        P("dp"),
        P("dp"),
        P(),
        P(None, "dp"),
        P(None, "dp"),
        P(None, "dp"),
        P(None, "dp", "tensor"),
        P(None, "dp", "tensor"),
        P(None, "dp", "tensor"),
        P(None, "tensor", "dp"),
        P(None, "tensor", "dp"),
        P(None, "tensor", "dp"),
    )
    out_specs = (
        P(),
        P(),
        P(None, "dp"),
        P(None, "dp"),
        P(None, "dp"),
        P(None, "dp"),
        P(None, "dp", "tensor"),
        P(None, "dp", "tensor"),
        P(None, "dp", "tensor"),
        P(None, "dp", "tensor"),
        P(None, "tensor", "dp"),
        P(None, "tensor", "dp"),
        P(None, "tensor", "dp"),
        P(None, "tensor", "dp"),
    )
    return jax.shard_map(
        on_device, mesh=mesh, in_specs=in_specs, out_specs=out_specs, check_vma=False
    )
```

profile of v0, /device:TPU:0, one launch (start us, length us, event | category | flops | bytes accessed | tf_op | source)
XLA Modules:
  0.0 1505.1 jit_solution(16987671061796512401)
XLA Ops:
  12.6 70.4 %all-gather.12.cloned.1.call-done = bf16[1,768,2496]{2,1,0:T(8,128)(2,1)} async-done(((bf16[1,96,2496]{2,1,0:T(8,128)(2,1)}), bf16[1,768,2496]{2,1,0:T(8,128)(2,1)}) %all-gather.12.cloned.1.call-update) | async-done | bytes 3833872 | tf_op jit(solution)/shard_map/all_gather | solution.py:76
  89.3 86.7 %all-gather.10.cloned.1.call-done = bf16[3592,768]{0,1:T(8,128)(2,1)} async-done(((bf16[3592,96]{0,1:T(8,128)(2,1)}), bf16[3592,768]{0,1:T(8,128)(2,1)}) %all-gather.10.cloned.1.call-update) | async-done | bytes 5517328 | tf_op jit(solution)/shard_map/all_gather | solution.py:208
  201.8 19.3 %all-gather.14.cloned.1.call-done = bf16[1,960,768]{1,2,0:T(8,128)(2,1)} async-done(((bf16[1,960,96]{1,2,0:T(8,128)(2,1)}), bf16[1,960,768]{1,2,0:T(8,128)(2,1)}) %all-gather.14.cloned.1.call-update) | async-done | bytes 1474576 | tf_op jit(solution)/shard_map/all_gather | solution.py:77
  224.7 40.6 %all-reduce.10.cloned.1.call-done = bf16[4,256,768]{2,1,0:T(8,128)(2,1)} async-done(((bf16[4,256,768]{2,1,0:T(8,128)(2,1)}), bf16[4,256,768]{2,1,0:T(8,128)(2,1)}) %all-reduce.10.cloned.1.call-update) | async-done | bytes 1572880 | tf_op jit(solution)/shard_map/psum | solution.py:82
  278.3 59.2 %all-gather.16.cloned.1.call-done = bf16[1,768,2496]{2,1,0:T(8,128)(2,1)} async-done(((bf16[1,96,2496]{2,1,0:T(8,128)(2,1)}), bf16[1,768,2496]{2,1,0:T(8,128)(2,1)}) %all-gather.16.cloned.1.call-update) | async-done | bytes 3833872 | tf_op jit(solution)/shard_map/all_gather | solution.py:76
  337.5 6.3 copy.173
  352.7 29.3 %all-reduce.12.cloned.1.call-done = bf16[4,256,768]{2,1,0:T(8,128)(2,1)} async-done(((bf16[4,256,768]{2,1,0:T(8,128)(2,1)}), bf16[4,256,768]{2,1,0:T(8,128)(2,1)}) %all-reduce.12.cloned.1.call-update) | async-done | bytes 1572880 | tf_op jit(solution)/shard_map/psum | solution.py:82
  400.0 28.5 %all-gather.18.cloned.1.call-done = bf16[1,960,768]{1,2,0:T(8,128)(2,1)} async-done(((bf16[1,960,96]{1,2,0:T(8,128)(2,1)}), bf16[1,960,768]{1,2,0:T(8,128)(2,1)}) %all-gather.18.cloned.1.call-update) | async-done | bytes 1474576 | tf_op jit(solution)/shard_map/all_gather | solution.py:77
  431.4 41.3 %all-reduce.14.cloned.1.call-done = bf16[4,256,768]{2,1,0:T(8,128)(2,1)} async-done(((bf16[4,256,768]{2,1,0:T(8,128)(2,1)}), bf16[4,256,768]{2,1,0:T(8,128)(2,1)}) %all-reduce.14.cloned.1.call-update) | async-done | bytes 1572880 | tf_op jit(solution)/shard_map/psum | solution.py:82
  488.0 39.4 %all-reduce.16.cloned.1.call-done = bf16[4,256,768]{2,1,0:T(8,128)(2,1)} async-done(((bf16[4,256,768]{2,1,0:T(8,128)(2,1)}), bf16[4,256,768]{2,1,0:T(8,128)(2,1)}) %all-reduce.16.cloned.1.call-update) | async-done | bytes 1572880 | tf_op jit(solution)/shard_map/psum | solution.py:82
  550.8 42.8 %all-reduce.18.cloned.1.call-done = bf16[4,256,768]{2,1,0:T(8,128)(2,1)} async-done(((bf16[4,256,768]{2,1,0:T(8,128)(2,1)}), bf16[4,256,768]{2,1,0:T(8,128)(2,1)}) %all-reduce.18.cloned.1.call-update) | async-done | bytes 1572880 | tf_op jit(solution)/shard_map/psum | solution.py:82
  621.1 43.0 %all-reduce.20.cloned.1.call-done = bf16[4,256,768]{2,1,0:T(8,128)(2,1)} async-done(((bf16[4,256,768]{2,1,0:T(8,128)(2,1)}), bf16[4,256,768]{2,1,0:T(8,128)(2,1)}) %all-reduce.20.cloned.1.call-update) | async-done | bytes 1572880 | tf_op jit(solution)/shard_map/psum | solution.py:82
  687.3 40.7 %all-reduce.22.cloned.1.call-done = bf16[4,256,768]{2,1,0:T(8,128)(2,1)} async-done(((bf16[4,256,768]{2,1,0:T(8,128)(2,1)}), bf16[4,256,768]{2,1,0:T(8,128)(2,1)}) %all-reduce.22.cloned.1.call-update) | async-done | bytes 1572880 | tf_op jit(solution)/shard_map/psum | solution.py:82
  777.9 8.4 concatenate.43
  803.4 9.5 concatenate.42
  816.7 11.1 psum.86
  846.3 12.3 copy.221
  863.7 9.6 reduce-scatter.20.cloned.1.call-done
  874.4 75.6 %reduce-scatter.18.cloned.1.call-done = f32[96,960]{1,0:T(8,128)} async-done(((f32[768,960]{1,0:T(8,128)}), f32[96,960]{1,0:T(8,128)}) %reduce-scatter.18.cloned.1.call-update) | async-done | bytes 368656
  952.1 140.8 %reduce-scatter.14.cloned.1.call-done = f32[96,2496]{1,0:T(8,128)} async-done(((f32[768,2496]{1,0:T(8,128)}), f32[96,2496]{1,0:T(8,128)}) %reduce-scatter.14.cloned.1.call-update) | async-done | bytes 958480 | tf_op jit(solution)/shard_map/reduce_scatter | solution.py:257
  1092.8 142.8 %reduce-scatter.12.cloned.1.call-done = f32[96,2496]{1,0:T(8,128)} async-done(((f32[768,2496]{1,0:T(8,128)}), f32[96,2496]{1,0:T(8,128)}) %reduce-scatter.12.cloned.1.call-update) | async-done | bytes 958480 | tf_op jit(solution)/shard_map/reduce_scatter | solution.py:257
  1238.2 191.0 %reduce-scatter.16.cloned.1.call-done = f32[96,3592]{1,0:T(8,128)} async-done(((f32[768,3592]{1,0:T(8,128)}), f32[96,3592]{1,0:T(8,128)}) %reduce-scatter.16.cloned.1.call-update) | async-done | bytes 1379344
  1436.0 39.6 %all-reduce = (f32[]{:T(128)}, f32[]{:T(128)}) all-reduce(f32[]{:T(128)S(6)} %div.194, f32[]{:T(128)S(6)} %add.343), channel_id=1, replica_groups=mesh['dp'=8,'tensor'=4] {'dp','tensor'}, use_global_device_ids=true, to_apply=%region_20.21 | all-reduce | flops 2 | bytes 16 | tf_op jit(solution)/shard_map/psum | solution.py:282
  1487.0 6.9 fusion.163
  (561 shorter events, 288.4 us)
Async XLA Ops:
  7.2 75.8 %all-gather.12.cloned.1.call-start = ((), (), s32[]{:S(2)}) async-start(), calls=%async_computation.16 | async-start | bytes 4423680 | tf_op jit(solution)/shard_map/all_gather | solution.py:76
  10.0 165.9 %all-gather.10.cloned.1.call-start = ((), (), s32[]{:S(2)}) async-start(), calls=%async_computation.5 | async-start | bytes 6414336 | tf_op jit(solution)/shard_map/all_gather | solution.py:208
  11.1 210.0 %all-gather.14.cloned.1.call-start = ((), (), s32[]{:S(2)}) async-start(), calls=%async_computation.17 | async-start | bytes 1769472 | tf_op jit(solution)/shard_map/all_gather | solution.py:77
  12.0 253.3 %all-reduce.10.cloned.1.call-start = ((), (), s32[]{:S(2)}) async-start(), calls=%async_computation.6 | async-start | bytes 3145728 | tf_op jit(solution)/shard_map/psum | solution.py:82
  12.4 180.2 %copy-start.12 = (f32[256,768]{1,0:T(8,128)}, f32[256,768]{1,0:T(8,128)S(1)}, u32[]{:S(2)}) copy-start(f32[256,768]{1,0:T(8,128)S(1)} %pad_maximum_fusion.4) | copy-start | bytes 2359300
  12.5 176.8 %copy-start.104 = (bf16[4,256,16]{1,2,0:T(8,128)(2,1)}, bf16[4,256,16]{1,2,0:T(8,128)(2,1)S(1)}, u32[]{:S(2)}) copy-start(bf16[4,256,16]{1,2,0:T(8,128)(2,1)S(1)} %fusion.119) | copy-start | bytes 98308
  12.6 163.4 %copy-start.151 = (bf16[4,128]{1,0:T(4,128)(2,1)}, bf16[4,128]{1,0:T(4,128)(2,1)S(1)}, u32[]{:S(2)}) copy-start(bf16[4,128]{1,0:T(4,128)(2,1)S(1)} %get-tuple-element.143) | copy-start | bytes 3076
  12.6 163.4 %copy-start.153 = (bf16[4,128]{1,0:T(4,128)(2,1)}, bf16[4,128]{1,0:T(4,128)(2,1)S(1)}, u32[]{:S(2)}) copy-start(bf16[4,128]{1,0:T(4,128)(2,1)S(1)} %get-tuple-element.144) | copy-start | bytes 3076
  12.6 166.6 %copy-start.157 = (s32[4]{0:T(128)S(1)}, s32[4]{0:T(128)}, u32[]{:S(2)}) copy-start(s32[4]{0:T(128)} %param.17) | copy-start | bytes 52
  201.8 63.5 %copy-start.52 = (bf16[4,3,64,256]{3,2,1,0:T(8,128)(2,1)}, bf16[4,3,64,256]{3,2,1,0:T(8,128)(2,1)S(1)}, u32[]{:S(2)}) copy-start(bf16[4,3,64,256]{3,2,1,0:T(8,128)(2,1)S(1)} %convolution_convert_fusion.15) | copy-start | bytes 1179652
  223.9 113.6 %all-gather.16.cloned.1.call-start = ((), (), s32[]{:S(2)}) async-start(), calls=%async_computation.18 | async-start | bytes 4423680 | tf_op jit(solution)/shard_map/all_gather | solution.py:76
  224.5 157.5 %all-reduce.12.cloned.1.call-start = ((), (), s32[]{:S(2)}) async-start(), calls=%async_computation.7 | async-start | bytes 3145728 | tf_op jit(solution)/shard_map/psum | solution.py:82
  277.5 150.9 %all-gather.18.cloned.1.call-start = ((), (), s32[]{:S(2)}) async-start(), calls=%async_computation.19 | async-start | bytes 1769472 | tf_op jit(solution)/shard_map/all_gather | solution.py:77
  278.2 194.5 %all-reduce.14.cloned.1.call-start = ((), (), s32[]{:S(2)}) async-start(), calls=%async_computation.8 | async-start | bytes 3145728 | tf_op jit(solution)/shard_map/psum | solution.py:82
  431.3 96.1 %all-reduce.16.cloned.1.call-start = ((), (), s32[]{:S(2)}) async-start(), calls=%async_computation.9 | async-start | bytes 3145728 | tf_op jit(solution)/shard_map/psum | solution.py:82
  484.3 109.3 %all-reduce.18.cloned.1.call-start = ((), (), s32[]{:S(2)}) async-start(), calls=%async_computation.10 | async-start | bytes 3145728 | tf_op jit(solution)/shard_map/psum | solution.py:82
  550.6 113.5 %all-reduce.20.cloned.1.call-start = ((), (), s32[]{:S(2)}) async-start(), calls=%async_computation.11 | async-start | bytes 3145728 | tf_op jit(solution)/shard_map/psum | solution.py:82
  621.0 106.9 %all-reduce.22.cloned.1.call-start = ((), (), s32[]{:S(2)}) async-start(), calls=%async_computation.12 | async-start | bytes 3145728 | tf_op jit(solution)/shard_map/psum | solution.py:82
  684.9 111.3 %all-reduce.24.cloned.1.call-start = ((), (), s32[]{:S(2)}) async-start(), calls=%async_computation.13 | async-start | bytes 3145728 | tf_op jit(solution)/shard_map/psum | solution.py:82
  752.2 121.0 %reduce-scatter.20.cloned.1.call-start = ((), (), s32[]{:S(2)}) async-start(), calls=%async_computation.22 | async-start | bytes 3538944
  759.2 190.8 %reduce-scatter.18.cloned.1.call-start = ((), (), s32[]{:S(2)}) async-start(), calls=%async_computation.21 | async-start | bytes 3538944
  767.5 325.3 %reduce-scatter.14.cloned.1.call-start = ((), (), s32[]{:S(2)}) async-start(), calls=%async_computation.15 | async-start | bytes 8847360 | tf_op jit(solution)/shard_map/reduce_scatter | solution.py:257
  786.4 449.2 %reduce-scatter.12.cloned.1.call-start = ((), (), s32[]{:S(2)}) async-start(), calls=%async_computation.14 | async-start | bytes 8847360 | tf_op jit(solution)/shard_map/reduce_scatter | solution.py:257
  812.9 616.3 %reduce-scatter.16.cloned.1.call-start = ((), (), s32[]{:S(2)}) async-start(), calls=%async_computation.20 | async-start | bytes 12828672
  (162 other events, 528.6 us)
Sparse Core Ops, SparseCore 0:
  10.8 72.1 all-gather.11
  85.8 90.1 all-gather.9
  178.7 42.3 all-gather.13
  224.0 41.2 all-reduce.9
  267.9 69.5 all-gather.15
  340.3 41.6 all-reduce.11
  384.2 44.2 all-gather.17
  431.5 41.2 all-reduce.13
  484.4 42.9 all-reduce.15
  550.7 42.8 all-reduce.17
  621.2 42.9 all-reduce.19
  685.0 42.8 all-reduce.21
  752.3 42.9 all-reduce.23
  798.7 74.4 reduce-scatter.19
  876.6 73.3 reduce-scatter.17
  953.5 139.2 reduce-scatter.13
  1096.3 139.2 reduce-scatter.11
  1239.2 189.9 reduce-scatter.15
where the time goes:
time: 1510 us
  waiting for transfers between devices  1100 us (73%)
  matrix products  130 us (9%)
  local copies, waits for them, and re-layouts  110 us (7%)
  other arithmetic  76.7 us (5%)
  blocking collectives  61.4 us (4%)
  between operations  21.8 us (1%)
    reduce_scatter x2, waiting for transfers between devices, on_device(): lax.psum_scatter(g_in, 'dp', scatter_dimension=0, tiled=True)  284 us
    unnamed x21, waiting for transfers between devices  278 us
    psum x8, waiting for transfers between devices, combine(): lax.psum(partial_value.astype(jnp.bfloat16), 'tensor').astype(jnp.float32)  277 us
    all_gather x2, waiting for transfers between devices, fetch_layer(): lax.all_gather(w_in[layer].astype(jnp.bfloat16), 'dp', axis=0, tiled=True)  130 us
    all_gather x1, waiting for transfers between devices, on_device(): lax.all_gather(stem.astype(jnp.bfloat16), 'dp', axis=1, tiled=True)  86.7 us
    unnamed x363, local copies, waits for them, and re-layouts  62.2 us
    all_gather x2, waiting for transfers between devices, fetch_layer(): lax.all_gather(w_out[layer].astype(jnp.bfloat16), 'dp', axis=1, tiled=True)  47.8 us
    dot_general x16, matrix products, matmul(): return jnp.dot(left, right, preferred_element_type=jnp.float32)  41.6 us
  transfers between devices with their start and end apart: 18, of which 17 were waited for; matrix products, arithmetic and copies ran while one was open for 11% of the time, Pallas kernels for 0%

commit v1 on v0

--- a/solution.py
+++ b/solution.py
@@ -79,7 +79,9 @@
 
 
 def combine(partial_value):
-    return lax.psum(partial_value.astype(jnp.bfloat16), "tensor").astype(jnp.float32)
+    return jnp.sum(lax.all_gather(partial_value.astype(jnp.bfloat16), "tensor"), axis=0).astype(
+        jnp.float32
+    )
 
 
 def attention_scores(qkv):

time: 1510 us -> 1570 us (1.040)
  other arithmetic: 76.7 us -> 119 us
    all_gather x0 -> x8, waiting for transfers between devices: none -> 303 us  [combine(): lax.all_gather(partial_value.astype(jnp.bfloat16), 'tensor')]
    psum x8 -> x0, waiting for transfers between devices: 277 us -> none  [combine(): lax.psum(partial_value.astype(jnp.bfloat16), 'tensor').astype(jnp.float32)]
    reduce_sum x0 -> x8, other arithmetic: none -> 42.7 us  [combine(): jnp.sum(lax.all_gather(partial_value.astype(jnp.bfloat16), 'tensor'), axi...]
    unnamed x363 -> x365, local copies, waits for them, and re-layouts: 62.2 us -> 63.7 us
  transfers between devices with their start and end apart: 18 -> 18, of which waited for: 17 -> 18; matrix products, arithmetic and copies ran while one was open for 11% -> 11% of each run, Pallas kernels for 0% -> 0%
where the time goes in v1:
time: 1570 us; the launch traced here: 1560 us
  waiting for transfers between devices  1110 us (71%)
  matrix products  129 us (8%)
  other arithmetic  119 us (8%)
  local copies, waits for them, and re-layouts  110 us (7%)
  blocking collectives  61.8 us (4%)
  between operations  22.1 us (1%)
    all_gather x8, waiting for transfers between devices, combine(): lax.all_gather(partial_value.astype(jnp.bfloat16), 'tensor')  303 us
    reduce_scatter x2, waiting for transfers between devices, on_device(): lax.psum_scatter(g_in, 'dp', scatter_dimension=0, tiled=True)  284 us
    unnamed x21, waiting for transfers between devices  273 us
    all_gather x2, waiting for transfers between devices, fetch_layer(): lax.all_gather(w_in[layer].astype(jnp.bfloat16), 'dp', axis=0, tiled=True)  124 us
    all_gather x1, waiting for transfers between devices, on_device(): lax.all_gather(stem.astype(jnp.bfloat16), 'dp', axis=1, tiled=True)  86.7 us
    unnamed x365, local copies, waits for them, and re-layouts  63.7 us
    all_gather x2, waiting for transfers between devices, fetch_layer(): lax.all_gather(w_out[layer].astype(jnp.bfloat16), 'dp', axis=1, tiled=True)  44.1 us
    reduce_sum x8, other arithmetic, combine(): jnp.sum(lax.all_gather(partial_value.astype(jnp.bfloat16), 'tensor'), axi...  42.7 us
  transfers between devices with their start and end apart: 18, of which 18 were waited for; matrix products, arithmetic and copies ran while one was open for 11% of the time, Pallas kernels for 0%

profile of v1, /device:TPU:0, one launch (start us, length us, event | category | flops | bytes accessed | tf_op | source)
XLA Modules:
  0.0 1559.4 jit_solution(16449888840358050372)
XLA Ops:
  12.6 70.4 %all-gather.32.cloned.1.call-done = bf16[1,768,2496]{2,1,0:T(8,128)(2,1)} async-done(((bf16[1,96,2496]{2,1,0:T(8,128)(2,1)}), bf16[1,768,2496]{2,1,0:T(8,128)(2,1)}) %all-gather.32.cloned.1.call-update) | async-done | bytes 3833872 | tf_op jit(solution)/shard_map/all_gather | solution.py:76
  83.0 6.3 copy.167
  89.3 86.7 %all-gather.22.cloned.1.call-done = bf16[3592,768]{0,1:T(8,128)(2,1)} async-done(((bf16[3592,96]{0,1:T(8,128)(2,1)}), bf16[3592,768]{0,1:T(8,128)(2,1)}) %all-gather.22.cloned.1.call-update) | async-done | bytes 5517328 | tf_op jit(solution)/shard_map/all_gather | solution.py:210
  200.4 20.6 %all-gather.34.cloned.1.call-done = bf16[1,960,768]{1,2,0:T(8,128)(2,1)} async-done(((bf16[1,960,96]{1,2,0:T(8,128)(2,1)}), bf16[1,960,768]{1,2,0:T(8,128)(2,1)}) %all-gather.34.cloned.1.call-update) | async-done | bytes 1474576 | tf_op jit(solution)/shard_map/all_gather | solution.py:77
  224.7 44.0 %all-gather.36.cloned.1.call-done = bf16[16,256,768]{2,1,0:T(8,128)(2,1)} async-done(((bf16[4,256,768]{2,1,0:T(8,128)(2,1)}), bf16[16,256,768]{2,1,0:T(8,128)(2,1)}) %all-gather.36.cloned.1.call-update) | async-done | bytes 6291472 | tf_op jit(solution)/shard_map/all_gather | solution.py:82
  287.1 53.8 %all-gather.38.cloned.1.call-done = bf16[1,768,2496]{2,1,0:T(8,128)(2,1)} async-done(((bf16[1,96,2496]{2,1,0:T(8,128)(2,1)}), bf16[1,768,2496]{2,1,0:T(8,128)(2,1)}) %all-gather.38.cloned.1.call-update) | async-done | bytes 3833872 | tf_op jit(solution)/shard_map/all_gather | solution.py:76
  340.9 6.2 copy.173
  356.2 31.9 %all-gather.24.cloned.1.call-done = bf16[4,4,256,768]{3,2,1,0:T(8,128)(2,1)} async-done(((bf16[1,4,256,768]{3,2,1,0:T(8,128)(2,1)}), bf16[4,4,256,768]{3,2,1,0:T(8,128)(2,1)}) %all-gather.24.cloned.1.call-update) | async-done | bytes 6291472 | tf_op jit(solution)/shard_map/all_gather | solution.py:82
  411.4 23.5 %all-gather.40.cloned.1.call-done = bf16[1,960,768]{1,2,0:T(8,128)(2,1)} async-done(((bf16[1,960,96]{1,2,0:T(8,128)(2,1)}), bf16[1,960,768]{1,2,0:T(8,128)(2,1)}) %all-gather.40.cloned.1.call-update) | async-done | bytes 1474576 | tf_op jit(solution)/shard_map/all_gather | solution.py:77
  438.3 44.4 %all-gather.42.cloned.1.call-done = bf16[16,256,768]{2,1,0:T(8,128)(2,1)} async-done(((bf16[4,256,768]{2,1,0:T(8,128)(2,1)}), bf16[16,256,768]{2,1,0:T(8,128)(2,1)}) %all-gather.42.cloned.1.call-update) | async-done | bytes 6291472 | tf_op jit(solution)/shard_map/all_gather | solution.py:82
  503.0 43.1 %all-gather.26.cloned.1.call-done = bf16[4,4,256,768]{3,2,1,0:T(8,128)(2,1)} async-done(((bf16[1,4,256,768]{3,2,1,0:T(8,128)(2,1)}), bf16[4,4,256,768]{3,2,1,0:T(8,128)(2,1)}) %all-gather.26.cloned.1.call-update) | async-done | bytes 6291472 | tf_op jit(solution)/shard_map/all_gather | solution.py:82
  574.9 46.3 %all-gather.28.cloned.1.call-done = bf16[4,4,256,768]{3,2,1,0:T(8,128)(2,1)} async-done(((bf16[1,4,256,768]{3,2,1,0:T(8,128)(2,1)}), bf16[4,4,256,768]{3,2,1,0:T(8,128)(2,1)}) %all-gather.28.cloned.1.call-update) | async-done | bytes 6291472 | tf_op jit(solution)/shard_map/all_gather | solution.py:82
  654.1 46.2 %all-gather.44.cloned.1.call-done = bf16[16,256,768]{2,1,0:T(8,128)(2,1)} async-done(((bf16[4,256,768]{2,1,0:T(8,128)(2,1)}), bf16[16,256,768]{2,1,0:T(8,128)(2,1)}) %all-gather.44.cloned.1.call-update) | async-done | bytes 6291472 | tf_op jit(solution)/shard_map/all_gather | solution.py:82
  726.9 46.0 %all-gather.30.cloned.1.call-done = bf16[4,4,256,768]{3,2,1,0:T(8,128)(2,1)} async-done(((bf16[1,4,256,768]{3,2,1,0:T(8,128)(2,1)}), bf16[4,4,256,768]{3,2,1,0:T(8,128)(2,1)}) %all-gather.30.cloned.1.call-update) | async-done | bytes 6291472 | tf_op jit(solution)/shard_map/all_gather | solution.py:82
  829.8 8.4 concatenate.43
  861.8 9.4 concatenate.42
  875.0 11.4 psum.22
  904.8 12.3 copy.221
  928.1 76.0 %reduce-scatter.18.cloned.1.call-done = f32[96,960]{1,0:T(8,128)} async-done(((f32[768,960]{1,0:T(8,128)}), f32[96,960]{1,0:T(8,128)}) %reduce-scatter.18.cloned.1.call-update) | async-done | bytes 368656
  1006.1 140.8 %reduce-scatter.14.cloned.1.call-done = f32[96,2496]{1,0:T(8,128)} async-done(((f32[768,2496]{1,0:T(8,128)}), f32[96,2496]{1,0:T(8,128)}) %reduce-scatter.14.cloned.1.call-update) | async-done | bytes 958480 | tf_op jit(solution)/shard_map/reduce_scatter | solution.py:259
  1146.9 142.8 %reduce-scatter.12.cloned.1.call-done = f32[96,2496]{1,0:T(8,128)} async-done(((f32[768,2496]{1,0:T(8,128)}), f32[96,2496]{1,0:T(8,128)}) %reduce-scatter.12.cloned.1.call-update) | async-done | bytes 958480 | tf_op jit(solution)/shard_map/reduce_scatter | solution.py:259
  1292.3 191.0 %reduce-scatter.16.cloned.1.call-done = f32[96,3592]{1,0:T(8,128)} async-done(((f32[768,3592]{1,0:T(8,128)}), f32[96,3592]{1,0:T(8,128)}) %reduce-scatter.16.cloned.1.call-update) | async-done | bytes 1379344
  1490.1 39.6 %all-reduce = (f32[]{:T(128)}, f32[]{:T(128)}) all-reduce(f32[]{:T(128)S(6)} %div.194, f32[]{:T(128)S(6)} %add.327), channel_id=1, replica_groups=mesh['dp'=8,'tensor'=4] {'dp','tensor'}, use_global_device_ids=true, to_apply=%region_20.21 | all-reduce | flops 2 | bytes 16 | tf_op jit(solution)/shard_map/psum | solution.py:284
  1541.1 6.9 fusion.163
  (570 shorter events, 329.6 us)
Async XLA Ops:
  7.2 75.8 %all-gather.32.cloned.1.call-start = ((), (), s32[]{:S(2)}) async-start(), calls=%async_computation.12 | async-start | bytes 4423680 | tf_op jit(solution)/shard_map/all_gather | solution.py:76
  10.0 165.9 %all-gather.22.cloned.1.call-start = ((), (), s32[]{:S(2)}) async-start(), calls=%async_computation.5 | async-start | bytes 6414336 | tf_op jit(solution)/shard_map/all_gather | solution.py:210
  11.1 210.0 %all-gather.34.cloned.1.call-start = ((), (), s32[]{:S(2)}) async-start(), calls=%async_computation.13 | async-start | bytes 1769472 | tf_op jit(solution)/shard_map/all_gather | solution.py:77
  12.0 256.8 %all-gather.36.cloned.1.call-start = ((), (), s32[]{:S(2)}) async-start(), calls=%async_computation.14 | async-start | bytes 7864320 | tf_op jit(solution)/shard_map/all_gather | solution.py:82
  12.3 165.5 %copy-start.152 = (bf16[4,128]{1,0:T(4,128)(2,1)}, bf16[4,128]{1,0:T(4,128)(2,1)S(1)}, u32[]{:S(2)}) copy-start(bf16[4,128]{1,0:T(4,128)(2,1)S(1)} %get-tuple-element.143) | copy-start | bytes 3076
  12.3 165.5 %copy-start.154 = (bf16[4,128]{1,0:T(4,128)(2,1)}, bf16[4,128]{1,0:T(4,128)(2,1)S(1)}, u32[]{:S(2)}) copy-start(bf16[4,128]{1,0:T(4,128)(2,1)S(1)} %get-tuple-element.144) | copy-start | bytes 3076
  12.4 163.5 %copy-start.105 = (bf16[4,256,16]{1,2,0:T(8,128)(2,1)}, bf16[4,256,16]{1,2,0:T(8,128)(2,1)S(1)}, u32[]{:S(2)}) copy-start(bf16[4,256,16]{1,2,0:T(8,128)(2,1)S(1)} %fusion.119) | copy-start | bytes 98308
  12.6 179.9 %copy-start.12 = (f32[256,768]{1,0:T(8,128)}, f32[256,768]{1,0:T(8,128)S(1)}, u32[]{:S(2)}) copy-start(f32[256,768]{1,0:T(8,128)S(1)} %pad_maximum_fusion.4) | copy-start | bytes 2359300
  89.3 92.8 %copy-start.158 = (s32[4]{0:T(128)S(1)}, s32[4]{0:T(128)}, u32[]{:S(2)}) copy-start(s32[4]{0:T(128)} %param.17) | copy-start | bytes 52
  200.4 73.6 %copy-start.53 = (bf16[4,3,64,256]{3,2,1,0:T(8,128)(2,1)}, bf16[4,3,64,256]{3,2,1,0:T(8,128)(2,1)S(1)}, u32[]{:S(2)}) copy-start(bf16[4,3,64,256]{3,2,1,0:T(8,128)(2,1)S(1)} %convolution_convert_fusion.15) | copy-start | bytes 1179652
  223.8 117.0 %all-gather.38.cloned.1.call-start = ((), (), s32[]{:S(2)}) async-start(), calls=%async_computation.15 | async-start | bytes 4423680 | tf_op jit(solution)/shard_map/all_gather | solution.py:76
  224.4 163.6 %all-gather.24.cloned.1.call-start = ((), (), s32[]{:S(2)}) async-start(), calls=%async_computation.6 | async-start | bytes 7864320 | tf_op jit(solution)/shard_map/all_gather | solution.py:82
  286.3 148.6 %all-gather.40.cloned.1.call-start = ((), (), s32[]{:S(2)}) async-start(), calls=%async_computation.16 | async-start | bytes 1769472 | tf_op jit(solution)/shard_map/all_gather | solution.py:77
  287.0 195.6 %all-gather.42.cloned.1.call-start = ((), (), s32[]{:S(2)}) async-start(), calls=%async_computation.17 | async-start | bytes 7864320 | tf_op jit(solution)/shard_map/all_gather | solution.py:82
  437.8 108.3 %all-gather.26.cloned.1.call-start = ((), (), s32[]{:S(2)}) async-start(), calls=%async_computation.7 | async-start | bytes 7864320 | tf_op jit(solution)/shard_map/all_gather | solution.py:82
  499.6 121.6 %all-gather.28.cloned.1.call-start = ((), (), s32[]{:S(2)}) async-start(), calls=%async_computation.8 | async-start | bytes 7864320 | tf_op jit(solution)/shard_map/all_gather | solution.py:82
  574.6 125.6 %all-gather.44.cloned.1.call-start = ((), (), s32[]{:S(2)}) async-start(), calls=%async_computation.18 | async-start | bytes 7864320 | tf_op jit(solution)/shard_map/all_gather | solution.py:82
  653.8 119.2 %all-gather.30.cloned.1.call-start = ((), (), s32[]{:S(2)}) async-start(), calls=%async_computation.9 | async-start | bytes 7864320 | tf_op jit(solution)/shard_map/all_gather | solution.py:82
  726.4 122.7 %all-gather.46.cloned.1.call-start = ((), (), s32[]{:S(2)}) async-start(), calls=%async_computation.19 | async-start | bytes 7864320 | tf_op jit(solution)/shard_map/all_gather | solution.py:82
  802.6 124.3 %reduce-scatter.20.cloned.1.call-start = ((), (), s32[]{:S(2)}) async-start(), calls=%async_computation.22 | async-start | bytes 3538944
  810.1 193.9 %reduce-scatter.18.cloned.1.call-start = ((), (), s32[]{:S(2)}) async-start(), calls=%async_computation.21 | async-start | bytes 3538944
  819.6 327.4 %reduce-scatter.14.cloned.1.call-start = ((), (), s32[]{:S(2)}) async-start(), calls=%async_computation.11 | async-start | bytes 8847360 | tf_op jit(solution)/shard_map/reduce_scatter | solution.py:259
  838.2 451.5 %reduce-scatter.12.cloned.1.call-start = ((), (), s32[]{:S(2)}) async-start(), calls=%async_computation.10 | async-start | bytes 8847360 | tf_op jit(solution)/shard_map/reduce_scatter | solution.py:259
  871.3 612.0 %reduce-scatter.16.cloned.1.call-start = ((), (), s32[]{:S(2)}) async-start(), calls=%async_computation.20 | async-start | bytes 12828672
  (163 other events, 557.6 us)
Sparse Core Ops, SparseCore 0:
  10.8 72.1 all-gather.31
  85.8 90.1 all-gather.21
  178.7 42.3 all-gather.33
  224.0 44.7 all-gather.35
  271.3 69.4 all-gather.37
  342.9 45.1 all-gather.23
  390.8 43.9 all-gather.39
  437.9 44.7 all-gather.41
  499.7 46.3 all-gather.25
  574.8 46.3 all-gather.27
  653.9 46.3 all-gather.43
  726.5 46.3 all-gather.29
  802.7 46.3 all-gather.45
  852.5 74.2 reduce-scatter.19
  930.3 73.7 reduce-scatter.17
  1007.6 139.3 reduce-scatter.13
  1150.4 139.2 reduce-scatter.11
  1293.3 189.9 reduce-scatter.15
